TPU v7x, 32 devices: a whole 2x2x4 slice. The times are simulated.
32 devices in a mesh: kpt: 2 (over y), row: 8 (over z, x), freq: 2 (over core).
Axes of the slice: x: 2, y: 2, z: 4, core: 2. Of those that a mesh axis runs over, the one named last changes fastest.
Arguments:
- screened: bfloat16 [8, 2, 8192, 8192], P(('kpt', 'freq'), None, 'row'), parts along dimension 0, may hold values from -0.0625 to 0.0625
- elements: bfloat16 [2, 1024, 8192], P(None, 'kpt', 'row'), parts along dimension 1, may hold values from -0.59765625 to 0.59765625
- node_freq: float32 [4], P('freq'), may hold values from 0.1 to 2
- node_weight: float32 [4], P('freq'), may hold values from 0.1 to 1
- band_energy: float32 [1024], P('kpt'), parts along dimension 0, may hold values from -1 to 1
- energy_grid: float32 [64], replicated, may hold values from -1 to 1
- pair_state: int32 [1024], P('kpt'), parts along dimension 0, may hold values from 0 to 31
- pair_band: int32 [1024], P('kpt'), parts along dimension 0, may hold values from 0 to 511
Outputs:
- sigma: float32 [2, 64, 64], P(None, 'kpt'), parts along dimension 1
There are 2 independent parts, one for each index of `kpt`. A program takes and returns all parts, laid end to end along the dimension named above; an argument that names none is the same for every part. Nothing has to cross between parts.
All inputs are finite; a program needn't handle non-finite values.
Results may differ from a plain program's by a relative error of at most 0.0003.
Values may be sent and summed in bfloat16 or wider, within the bound.
A program may use at most 192 MiB of HBM per device.

v0:
```python
import jax
import jax.numpy as jnp
from jax import lax
from jax.sharding import PartitionSpec as P

NSTATE = 32


def product(weights, piece):
    return jnp.einsum("jgc,pc->jgp", weights, piece, preferred_element_type=jnp.float32)


def self_energy(
    form_re, form_im, node_freq, node_weight, band_energy, energy_grid, pair_state, pair_band
):
    band_onehot = (
        pair_band[:, None] == jnp.arange(band_energy.shape[0], dtype=jnp.int32)[None, :]
    ).astype(jnp.float32)
    pair_eps = jnp.dot(band_onehot, band_energy, precision=lax.Precision.HIGHEST)
    delta = energy_grid[None, :] - pair_eps[:, None]
    factor = (
        node_weight[:, None, None]
        * delta[None]
        / (delta[None] ** 2 + node_freq[:, None, None] ** 2)
    )
    terms_re = jnp.sum(form_re[:, :, None] * factor, axis=0)
    terms_im = jnp.sum(form_im[:, :, None] * factor, axis=0)
    state_onehot = (jnp.arange(NSTATE, dtype=jnp.int32)[:, None] == pair_state[None, :]).astype(
        jnp.float32
    )
    sig_re = jnp.dot(state_onehot, terms_re, precision=lax.Precision.HIGHEST)
    sig_im = jnp.dot(state_onehot, terms_im, precision=lax.Precision.HIGHEST)
    return jnp.stack([sig_re, sig_im])


def per_device(
    screened, elements, node_freq, node_weight, band_energy, energy_grid, pair_state, pair_band
):
    w_real = screened[:, 0]
    w_imag = screened[:, 1]
    npair = elements.shape[1]
    half = npair // lax.axis_size("freq")
    mine = lax.dynamic_slice_in_dim(elements, lax.axis_index("freq") * half, half, 1)
    collected = lax.all_gather(mine, "row", axis=2, tiled=True)
    piece = lax.all_gather(collected, "freq", axis=1, tiled=True)
    part_real = product(w_real, piece[0]) - product(w_imag, piece[1])
    part_imag = product(w_real, piece[1]) + product(w_imag, piece[0])
    stacked = jnp.stack([part_real, part_imag])
    y_real = stacked[0]
    y_imag = stacked[1]
    own_real = elements[0].T.astype(jnp.float32)[None]
    own_imag = elements[1].T.astype(jnp.float32)[None]
    form_re = jnp.sum(own_real * y_real + own_imag * y_imag, axis=1)
    form_im = jnp.sum(own_real * y_imag - own_imag * y_real, axis=1)
    form_re, form_im = lax.psum((form_re, form_im), "row")
    partial_sigma = self_energy(
        form_re, form_im, node_freq, node_weight, band_energy, energy_grid, pair_state, pair_band
    )
    return lax.psum(partial_sigma, "freq")


def solution(mesh):
    in_specs = (
        P(("kpt", "freq"), None, "row", None),
        P(None, "kpt", "row"),
        P("freq"),
        P("freq"),
        P("kpt"),
        P(),
        P("kpt"),
        P("kpt"),
    )
    out_specs = P(None, "kpt", None)
    return jax.shard_map(
        per_device, mesh=mesh, in_specs=in_specs, out_specs=out_specs, check_vma=False
    )
```

profile of v0, /device:TPU:0, one launch (start us, length us, event | category | flops | bytes accessed | tf_op | source)
XLA Modules:
  0.0 302.2 jit_solution(1204558639361420559)
XLA Ops:
  6.5 0.0 copy-start
  6.5 0.0 copy-start.1
  6.5 0.0 copy-start.10
  6.5 0.0 copy-start.9
  6.5 0.0 copy-start.6
  6.5 0.0 all-gather.3.cloned.1.call-start
  6.6 2.4 constant_dynamic-slice_fusion
  9.0 0.0 all-gather.3.cloned.1.call-update
  9.0 0.0 all-gather.5.cloned.1.call-start
  9.1 127.7 %all-gather.3.cloned.1.call-done = bf16[2,256,8192]{2,1,0:T(8,128)(2,1)} async-done(((bf16[2,256,1024]{2,1,0:T(8,128)(2,1)}), bf16[2,256,8192]{2,1,0:T(8,128)(2,1)}) %all-gather.3.cloned.1.call-update) | async-done | bytes 8388624 | tf_op jit(solution)/shard_map/all_gather | solution.py:44
  136.8 0.0 all-gather.5.cloned.1.call-update
  136.8 0.0 copy-done.10
  136.8 0.5 integer_pow.13
  137.3 0.0 copy-done
  137.3 0.0 copy-done.9
  137.3 0.6 fusion.16
  137.9 0.0 copy-done.6
  137.9 0.8 broadcast_subtract_fusion
  138.7 0.0 copy-done.1
  138.7 2.5 convert_bitcast_fusion.1
  141.2 25.4 %all-gather.5.cloned.1.call-done = bf16[2,512,8192]{2,1,0:T(8,128)(2,1)} async-done(((bf16[2,256,8192]{2,1,0:T(8,128)(2,1)}), bf16[2,512,8192]{2,1,0:T(8,128)(2,1)}) %all-gather.5.cloned.1.call-update) | async-done | bytes 16777232 | tf_op jit(solution)/shard_map/all_gather | solution.py:45
  166.6 24.9 %fusion = f32[512,2,1024]{2,0,1:T(8,128)} fusion(bf16[2,2,1024,8192]{3,2,1,0:T(8,128)(2,1)} %param.8, bf16[2,512,8192]{2,1,0:T(8,128)(2,1)} %all-gather.5.cloned.1.call-done), kind=kOutput, calls=%fused_computation | convolution fusion | flops 17179869184 | bytes 46137344 | tf_op jit(solution)/shard_map/jgc,pc->jgp/dot_general | solution.py:10
  191.5 24.9 %fusion.2 = f32[512,2,1024]{2,0,1:T(8,128)} fusion(bf16[2,2,1024,8192]{3,2,1,0:T(8,128)(2,1)} %param.8, bf16[2,512,8192]{2,1,0:T(8,128)(2,1)} %all-gather.5.cloned.1.call-done), kind=kOutput, calls=%fused_computation.2 | convolution fusion | flops 17179869184 | bytes 46137344 | tf_op jit(solution)/shard_map/jgc,pc->jgp/dot_general | solution.py:10
  216.5 0.0 copy-start.2
  216.5 25.1 %fusion.6 = f32[512,2,1024]{2,0,1:T(8,128)} fusion(bf16[2,2,1024,8192]{3,2,1,0:T(8,128)(2,1)} %param.8, bf16[2,512,8192]{2,1,0:T(8,128)(2,1)} %all-gather.5.cloned.1.call-done), kind=kOutput, calls=%fused_computation.6 | convolution fusion | flops 17179869184 | bytes 46137344 | tf_op jit(solution)/shard_map/jgc,pc->jgp/dot_general | solution.py:10
  241.5 0.0 copy-done.2
  241.5 0.0 copy-start.3
  241.6 0.0 copy-start.4
  241.6 0.0 copy-start.7
  241.6 0.0 copy-start.8
  241.6 0.0 copy-start.5
  241.6 27.3 %fusion.13 = (f32[2,512]{1,0:T(2,128)S(1)}, f32[2,512]{1,0:T(2,128)S(1)}) fusion(f32[1024,512]{0,1:T(8,128)} %get-tuple-element.12, f32[1024,512]{0,1:T(8,128)S(1)} %copy-done.2, f32[512,2,1024]{2,0,1:T(8,128)} %fusion, f32[512,2,1024]{2,0,1:T(8,128)} %fusion.6, f32[512,2,1024]{2,0,1:T(8,128)} %fusion.2, bf16[2,2,1024,8192]{3,2,1,0:T(8,128)(2,1)} %param.8, ...), kind=kOutput, calls=%fused_computation.17 | convolution fusion | flops 17190354944 | bytes 58728448 | tf_op jit(solution)/shard_map/jgc,pc->jgp/dot_general | solution.py:10
  268.9 21.9 %all-reduce = (f32[2,512]{1,0:T(2,128)S(1)}, f32[2,512]{1,0:T(2,128)S(1)}) all-reduce(f32[2,512]{1,0:T(2,128)S(1)} %get-tuple-element.5, f32[2,512]{1,0:T(2,128)S(1)} %get-tuple-element.6), channel_id=1, replica_groups=mesh['kpt'=2,'row'=8,'freq'=2] {'row'}, use_global_device_ids=true, to_apply=%region_1.0 | all-reduce | flops 2048 | bytes 16384 | tf_op jit(solution)/shard_map/psum | solution.py:55
  290.8 0.0 copy-done.3
  290.8 0.0 copy-done.4
  290.8 0.0 copy-done.7
  290.8 0.0 copy-done.8
  290.8 0.1 multiply_reduce_fusion.1
  291.0 0.0 copy-done.5
  291.0 0.2 convolution_bitcast_fusion
  291.2 0.2 convolution_bitcast_fusion.1
  291.4 4.0 %psum.23 = f32[2,32,64]{2,1,0:T(8,128)} all-reduce(f32[2,32,64]{2,1,0:T(8,128)S(1)} %pad_maximum_fusion), channel_id=1, replica_groups=mesh['kpt'=2,'row'=8,'freq'=2] {'freq'}, use_global_device_ids=true, to_apply=%region_6.0 | all-reduce | flops 4096 | bytes 32768 | tf_op jit(solution)/shard_map/psum | solution.py:59
  (1 shorter events, 0.0 us)
Async XLA Ops:
  6.5 130.8 %copy-start = (f32[512]{0:T(512)S(1)}, f32[512]{0:T(512)}, u32[]{:S(2)}) copy-start(f32[512]{0:T(512)} %param.12) | copy-start | bytes 6148
  6.5 132.2 %copy-start.1 = (bf16[2,512,1024]{2,1,0:T(8,128)(2,1)S(1)}, bf16[2,512,1024]{2,1,0:T(8,128)(2,1)}, u32[]{:S(2)}) copy-start(bf16[2,512,1024]{2,1,0:T(8,128)(2,1)} %param.9) | copy-start | bytes 6291460
  6.5 130.2 %copy-start.10 = (f32[2]{0:T(128)S(1)}, f32[2]{0:T(128)}, u32[]{:S(2)}) copy-start(f32[2]{0:T(128)} %param.10) | copy-start | bytes 28
  6.5 130.8 %copy-start.9 = (s32[512]{0:T(512)S(1)}, s32[512]{0:T(512)}, u32[]{:S(2)}) copy-start(s32[512]{0:T(512)} %param.15) | copy-start | bytes 6148
  6.5 131.4 %copy-start.6 = (f32[64]{0:T(128)S(1)}, f32[64]{0:T(128)}, u32[]{:S(2)}) copy-start(f32[64]{0:T(128)} %param.13) | copy-start | bytes 772
  6.5 130.2 %all-gather.3.cloned.1.call-start = ((), (), s32[]{:S(2)}) async-start(), calls=%async_computation | async-start | bytes 9437184 | tf_op jit(solution)/shard_map/all_gather | solution.py:44
  9.0 157.6 %all-gather.5.cloned.1.call-start = ((), (), s32[]{:S(2)}) async-start(), calls=%async_computation.1 | async-start | bytes 25165824 | tf_op jit(solution)/shard_map/all_gather | solution.py:45
  216.5 25.1 %copy-start.2 = (f32[1024,512]{0,1:T(8,128)S(1)}, f32[1024,512]{0,1:T(8,128)}, u32[]{:S(2)}) copy-start(f32[1024,512]{0,1:T(8,128)} %get-tuple-element.11) | copy-start | bytes 6291460
  241.5 49.2 %copy-start.3 = (f32[512,64]{0,1:T(8,128)S(1)}, f32[512,64]{0,1:T(8,128)}, u32[]{:S(2)}) copy-start(f32[512,64]{0,1:T(8,128)} %get-tuple-element.13) | copy-start | bytes 393220
  241.6 49.2 %copy-start.4 = (f32[512,64]{0,1:T(8,128)S(1)}, f32[512,64]{0,1:T(8,128)}, u32[]{:S(2)}) copy-start(f32[512,64]{0,1:T(8,128)} %get-tuple-element.14) | copy-start | bytes 393220
  241.6 49.3 %copy-start.7 = (f32[2]{0:T(128)S(1)}, f32[2]{0:T(128)}, u32[]{:S(2)}) copy-start(f32[2]{0:T(128)} %param.11) | copy-start | bytes 28
  241.6 49.3 %copy-start.8 = (f32[2]{0:T(128)S(1)}, f32[2]{0:T(128)}, u32[]{:S(2)}) copy-start(f32[2]{0:T(128)} %integer_pow.13) | copy-start | bytes 28
  241.6 49.4 %copy-start.5 = (s32[512]{0:T(512)S(1)}, s32[512]{0:T(512)}, u32[]{:S(2)}) copy-start(s32[512]{0:T(512)} %param.14) | copy-start | bytes 6148
Sparse Core Ops, SparseCore 0:
  9.5 127.1 all-gather.2
  138.3 28.2 all-gather.4
where the time goes:
time: 302 us
  waiting for transfers between devices  153 us (51%)
  matrix products  103 us (34%)
  blocking collectives  25.9 us (9%)
  between operations  13.5 us (4%)
  other arithmetic  3.93 us (1%)
    all_gather x1, waiting for transfers between devices, per_device(): collected = lax.all_gather(mine, 'row', axis=2, tiled=True)  128 us
    dot_general x4, matrix products, product(): jnp.einsum('jgc,pc->jgp', weights, piece, preferred_element_type=jnp.floa...  102 us
    all_gather x1, waiting for transfers between devices, per_device(): piece = lax.all_gather(collected, 'freq', axis=1, tiled=True)  25.4 us
    psum x1, blocking collectives, per_device(): form_re, form_im = lax.psum((form_re, form_im), 'row')  21.9 us
  transfers between devices with their start and end apart: 2, of which 2 were waited for; matrix products, arithmetic and copies ran while one was open for 1% of the time, Pallas kernels for 0%

commit v1 on v0

--- a/solution.py
+++ b/solution.py
@@ -36,12 +36,25 @@
 def per_device(
     screened, elements, node_freq, node_weight, band_energy, energy_grid, pair_state, pair_band
 ):
+
+    def _time_roads(load):
+        n_all = lax.psum(1, "row")
+        answer = [(b - 1, b) for b in range(1, n_all)] + [(n_all - 1, 0)]
+        passed = load
+        stack_in = [passed]
+        for _ in range(n_all - 1):
+            passed = lax.ppermute(passed, axis_name="row", perm=answer)
+            stack_in += [passed]
+        f_next = jnp.concatenate([*reversed(stack_in)], 2)
+        block_last = jnp.roll(f_next, (lax.axis_index("row") + 1) * passed.shape[2], axis=2)
+        return block_last
+
     w_real = screened[:, 0]
     w_imag = screened[:, 1]
     npair = elements.shape[1]
     half = npair // lax.axis_size("freq")
     mine = lax.dynamic_slice_in_dim(elements, lax.axis_index("freq") * half, half, 1)
-    collected = lax.all_gather(mine, "row", axis=2, tiled=True)
+    collected = _time_roads(mine)
     piece = lax.all_gather(collected, "freq", axis=1, tiled=True)
     part_real = product(w_real, piece[0]) - product(w_imag, piece[1])
     part_imag = product(w_real, piece[1]) + product(w_imag, piece[0])

time: 302 us -> 388 us (1.28)
  waiting for transfers between devices: 153 us -> 197 us
  local copies, waits for them, and re-layouts: 2.45 us -> 39.7 us
    ppermute x0 -> x7, waiting for transfers between devices: none -> 176 us  [_time_roads(): passed = lax.ppermute(passed, axis_name='row', perm=answer)]
    all_gather x1 -> x0, waiting for transfers between devices: 128 us -> none  [per_device(): collected = lax.all_gather(mine, 'row', axis=2, tiled=True)]
    unnamed x22 -> x55, local copies, waits for them, and re-layouts: 0.05 us -> 29.6 us
    dynamic_slice x0 -> x1, local copies, waits for them, and re-layouts: none -> 7.6 us  [_time_roads(): jnp.roll(f_next, (lax.axis_index('row') + 1) * passed.shape[2], axis=2)]
    all_gather x1, waiting for transfers between devices: 25.4 us -> 21.3 us  [per_device(): piece = lax.all_gather(collected, 'freq', axis=1, tiled=True)]
  transfers between devices with their start and end apart: 2 -> 8, of which waited for: 2 -> 8; matrix products, arithmetic and copies ran while one was open for 1% -> 1% of each run, Pallas kernels for 0% -> 0%
where the time goes in v1:
time: 388 us; the launch traced here: 387 us
  waiting for transfers between devices  197 us (51%)
  matrix products  103 us (27%)
  local copies, waits for them, and re-layouts  39.7 us (10%)
  blocking collectives  25.9 us (7%)
  between operations  13.6 us (4%)
  other arithmetic  4.57 us (1%)
    ppermute x7, waiting for transfers between devices, _time_roads(): passed = lax.ppermute(passed, axis_name='row', perm=answer)  176 us
    dot_general x4, matrix products, product(): jnp.einsum('jgc,pc->jgp', weights, piece, preferred_element_type=jnp.floa...  102 us
    unnamed x55, local copies, waits for them, and re-layouts  29.6 us
    psum x1, blocking collectives, per_device(): form_re, form_im = lax.psum((form_re, form_im), 'row')  21.9 us
    all_gather x1, waiting for transfers between devices, per_device(): piece = lax.all_gather(collected, 'freq', axis=1, tiled=True)  21.3 us
  transfers between devices with their start and end apart: 8, of which 8 were waited for; matrix products, arithmetic and copies ran while one was open for 1% of the time, Pallas kernels for 0%

profile of v1, /device:TPU:0, one launch (start us, length us, event | category | flops | bytes accessed | tf_op | source)
XLA Modules:
  0.0 387.2 jit_solution(2989809023601234066)
XLA Ops:
  6.5 0.0 copy-start
  6.5 0.0 all-gather.2.cloned.1.call-start
  6.5 1.4 constant_dynamic-slice_fusion.1
  8.0 3.0 collective-permute-start
  11.0 26.2 %collective-permute-done = bf16[2,256,1024]{2,1,0:T(8,128)(2,1)S(1)} collective-permute-done((bf16[2,256,1024]{2,1,0:T(8,128)(2,1)S(1)}, bf16[2,256,1024]{2,1,0:T(8,128)(2,1)S(1)}, u32[]{:S(2)}, u32[]{:S(2)}) %collective-permute-start) | collective-permute-done | bytes 1048608 | tf_op jit(solution)/shard_map/ppermute | solution.py:46
  37.2 0.0 collective-permute-start.1
  37.2 27.0 %collective-permute-done.1 = bf16[2,256,1024]{2,1,0:T(8,128)(2,1)S(1)} collective-permute-done((bf16[2,256,1024]{2,1,0:T(8,128)(2,1)S(1)}, bf16[2,256,1024]{2,1,0:T(8,128)(2,1)S(1)}, u32[]{:S(2)}, u32[]{:S(2)}) %collective-permute-start.1) | collective-permute-done | bytes 1048608 | tf_op jit(solution)/shard_map/ppermute | solution.py:46
  64.2 1.0 copy-done.3
  65.2 0.0 collective-permute-start.2
  65.2 26.2 %collective-permute-done.2 = bf16[2,256,1024]{2,1,0:T(8,128)(2,1)S(1)} collective-permute-done((bf16[2,256,1024]{2,1,0:T(8,128)(2,1)S(1)}, bf16[2,256,1024]{2,1,0:T(8,128)(2,1)S(1)}, u32[]{:S(2)}, u32[]{:S(2)}) %collective-permute-start.2) | collective-permute-done | bytes 1048608 | tf_op jit(solution)/shard_map/ppermute | solution.py:46
  91.4 1.0 copy-done.5
  92.4 0.0 collective-permute-start.3
  92.4 25.3 %collective-permute-done.3 = bf16[2,256,1024]{2,1,0:T(8,128)(2,1)S(1)} collective-permute-done((bf16[2,256,1024]{2,1,0:T(8,128)(2,1)S(1)}, bf16[2,256,1024]{2,1,0:T(8,128)(2,1)S(1)}, u32[]{:S(2)}, u32[]{:S(2)}) %collective-permute-start.3) | collective-permute-done | bytes 1048608 | tf_op jit(solution)/shard_map/ppermute | solution.py:46
  117.7 1.0 copy-done.7
  118.7 0.0 collective-permute-start.4
  118.7 24.4 %collective-permute-done.4 = bf16[2,256,1024]{2,1,0:T(8,128)(2,1)S(1)} collective-permute-done((bf16[2,256,1024]{2,1,0:T(8,128)(2,1)S(1)}, bf16[2,256,1024]{2,1,0:T(8,128)(2,1)S(1)}, u32[]{:S(2)}, u32[]{:S(2)}) %collective-permute-start.4) | collective-permute-done | bytes 1048608 | tf_op jit(solution)/shard_map/ppermute | solution.py:46
  143.1 1.0 copy-done.9
  144.1 0.0 collective-permute-start.5
  144.1 23.7 %collective-permute-done.5 = bf16[2,256,1024]{2,1,0:T(8,128)(2,1)} collective-permute-done((bf16[2,256,1024]{2,1,0:T(8,128)(2,1)S(1)}, bf16[2,256,1024]{2,1,0:T(8,128)(2,1)}, u32[]{:S(2)}, u32[]{:S(2)}) %collective-permute-start.5) | collective-permute-done | bytes 1048608 | tf_op jit(solution)/shard_map/ppermute | solution.py:46
  167.8 0.0 collective-permute-start.6
  167.8 0.0 copy-start.4
  167.9 23.0 %collective-permute-done.6 = bf16[2,256,1024]{2,1,0:T(8,128)(2,1)} collective-permute-done((bf16[2,256,1024]{2,1,0:T(8,128)(2,1)}, bf16[2,256,1024]{2,1,0:T(8,128)(2,1)}, u32[]{:S(2)}, u32[]{:S(2)}) %collective-permute-start.6) | collective-permute-done | bytes 1048608 | tf_op jit(solution)/shard_map/ppermute | solution.py:46
  190.9 2.3 constant_dynamic-update-slice_fusion.15
  193.2 2.3 constant_dynamic-update-slice_fusion.14
  195.5 2.2 constant_dynamic-update-slice_fusion.13
  197.7 2.3 constant_dynamic-update-slice_fusion.12
  200.0 2.3 constant_dynamic-update-slice_fusion.11
  202.3 2.3 constant_dynamic-update-slice_fusion.10
  204.6 1.0 constant_dynamic-update-slice_fusion.9
  205.6 0.0 copy-done.2
  205.6 1.0 constant_dynamic-update-slice_fusion.8
  206.7 2.3 constant_dynamic-update-slice_fusion.7
  208.9 2.3 constant_dynamic-update-slice_fusion.6
  211.2 0.0 copy-done.10
  211.2 1.0 constant_dynamic-update-slice_fusion.5
  212.2 0.0 copy-done.8
  212.2 1.0 constant_dynamic-update-slice_fusion.4
  213.3 0.0 copy-done.6
  213.3 1.1 constant_dynamic-update-slice_fusion.3
  214.4 0.0 copy-done.4
  214.4 1.1 constant_dynamic-update-slice_fusion.2
  215.4 1.1 constant_dynamic-update-slice_fusion.1
  216.5 1.1 constant_dynamic-update-slice_fusion
  217.6 7.6 %constant_dynamic-slice_fusion = bf16[2,256,8192]{2,1,0:T(8,128)(2,1)} fusion(bf16[2,256,16384]{2,1,0:T(8,128)(2,1)} %constant_dynamic-update-slice_fusion, s32[]{:T(128)S(6)} %select_n.18), kind=kLoop, calls=%fused_computation.54 | loop fusion | bytes 16777220 | tf_op jit(solution)/shard_map/jit(_roll_dynamic)/dynamic_slice | solution.py:49
  225.2 0.0 all-gather.2.cloned.1.call-update
  225.2 0.5 integer_pow.13
  225.7 0.0 copy-done.18
  225.7 0.6 fusion.16
  226.3 0.8 broadcast_subtract_fusion
  227.1 3.1 convert_bitcast_fusion.1
  230.3 21.3 %all-gather.2.cloned.1.call-done = bf16[2,512,8192]{2,1,0:T(8,128)(2,1)} async-done(((bf16[2,256,8192]{2,1,0:T(8,128)(2,1)}), bf16[2,512,8192]{2,1,0:T(8,128)(2,1)}) %all-gather.2.cloned.1.call-update) | async-done | bytes 16777232 | tf_op jit(solution)/shard_map/all_gather | solution.py:58
  251.5 24.9 %fusion = f32[512,2,1024]{2,0,1:T(8,128)} fusion(bf16[2,2,1024,8192]{3,2,1,0:T(8,128)(2,1)} %param.8, bf16[2,512,8192]{2,1,0:T(8,128)(2,1)} %all-gather.2.cloned.1.call-done), kind=kOutput, calls=%fused_computation | convolution fusion | flops 17179869184 | bytes 46137344 | tf_op jit(solution)/shard_map/jgc,pc->jgp/dot_general | solution.py:10
  276.5 24.9 %fusion.2 = f32[512,2,1024]{2,0,1:T(8,128)} fusion(bf16[2,2,1024,8192]{3,2,1,0:T(8,128)(2,1)} %param.8, bf16[2,512,8192]{2,1,0:T(8,128)(2,1)} %all-gather.2.cloned.1.call-done), kind=kOutput, calls=%fused_computation.2 | convolution fusion | flops 17179869184 | bytes 46137344 | tf_op jit(solution)/shard_map/jgc,pc->jgp/dot_general | solution.py:10
  301.4 25.1 %fusion.6 = f32[512,2,1024]{2,0,1:T(8,128)} fusion(bf16[2,2,1024,8192]{3,2,1,0:T(8,128)(2,1)} %param.8, bf16[2,512,8192]{2,1,0:T(8,128)(2,1)} %all-gather.2.cloned.1.call-done), kind=kOutput, calls=%fused_computation.6 | convolution fusion | flops 17179869184 | bytes 46137344 | tf_op jit(solution)/shard_map/jgc,pc->jgp/dot_general | solution.py:10
  326.5 0.0 copy-start.16
  326.5 0.0 copy-start.17
  326.5 0.0 copy-start.14
  326.5 0.0 copy-start.1
  326.5 27.3 %fusion.13 = (f32[2,512]{1,0:T(2,128)S(1)}, f32[2,512]{1,0:T(2,128)S(1)}) fusion(f32[1024,512]{0,1:T(8,128)} %get-tuple-element.12, f32[1024,512]{0,1:T(8,128)S(1)} %copy-done.11, f32[512,2,1024]{2,0,1:T(8,128)} %fusion, f32[512,2,1024]{2,0,1:T(8,128)} %fusion.6, f32[512,2,1024]{2,0,1:T(8,128)} %fusion.2, bf16[2,2,1024,8192]{3,2,1,0:T(8,128)(2,1)} %param.8, ...), kind=kOutput, calls=%fused_computation.17 | convolution fusion | flops 17190354944 | bytes 58728448 | tf_op jit(solution)/shard_map/jgc,pc->jgp/dot_general | solution.py:10
  353.9 21.9 %all-reduce = (f32[2,512]{1,0:T(2,128)S(1)}, f32[2,512]{1,0:T(2,128)S(1)}) all-reduce(f32[2,512]{1,0:T(2,128)S(1)} %get-tuple-element.5, f32[2,512]{1,0:T(2,128)S(1)} %get-tuple-element.6), channel_id=1, replica_groups=mesh['kpt'=2,'row'=8,'freq'=2] {'row'}, use_global_device_ids=true, to_apply=%region_1.2 | all-reduce | flops 2048 | bytes 16384 | tf_op jit(solution)/shard_map/psum | solution.py:68
  375.8 0.1 multiply_reduce_fusion.1
  376.0 0.2 convolution_bitcast_fusion
  376.2 0.2 convolution_bitcast_fusion.1
  376.4 4.0 %psum.23 = f32[2,32,64]{2,1,0:T(8,128)} all-reduce(f32[2,32,64]{2,1,0:T(8,128)S(1)} %pad_maximum_fusion), channel_id=1, replica_groups=mesh['kpt'=2,'row'=8,'freq'=2] {'freq'}, use_global_device_ids=true, to_apply=%region_6.7 | all-reduce | flops 4096 | bytes 32768 | tf_op jit(solution)/shard_map/psum | solution.py:72
  (25 shorter events, 0.0 us)
Async XLA Ops:
  6.5 219.2 %copy-start = (f32[512]{0:T(512)S(1)}, f32[512]{0:T(512)}, u32[]{:S(2)}) copy-start(f32[512]{0:T(512)} %param.12) | copy-start | bytes 6148
  6.5 199.1 %copy-start.2 = (bf16[2,512,1024]{2,1,0:T(8,128)(2,1)S(1)}, bf16[2,512,1024]{2,1,0:T(8,128)(2,1)}, u32[]{:S(2)}) copy-start(bf16[2,512,1024]{2,1,0:T(8,128)(2,1)} %param.9) | copy-start | bytes 6291460
  6.5 245.0 %all-gather.2.cloned.1.call-start = ((), (), s32[]{:S(2)}) async-start(), calls=%async_computation | async-start | bytes 25165824 | tf_op jit(solution)/shard_map/all_gather | solution.py:58
  8.0 29.2 %collective-permute-start = (bf16[2,256,1024]{2,1,0:T(8,128)(2,1)S(1)}, bf16[2,256,1024]{2,1,0:T(8,128)(2,1)S(1)}, u32[]{:S(2)}, u32[]{:S(2)}) collective-permute-start(bf16[2,256,1024]{2,1,0:T(8,128)(2,1)S(1)} %constant_dynamic-slice_fusion.1), channel_id=1, source_target_pairs={{0,2},{2,4},{4,6},{6,8},{8,10},{10,12},{12,14},{14,0},{1,3},{3,5},... | collective-permute-start | bytes 3145736 | tf_op jit(solution)/shard_map/ppermute | solution.py:46
  37.2 27.0 %collective-permute-start.1 = (bf16[2,256,1024]{2,1,0:T(8,128)(2,1)S(1)}, bf16[2,256,1024]{2,1,0:T(8,128)(2,1)S(1)}, u32[]{:S(2)}, u32[]{:S(2)}) collective-permute-start(bf16[2,256,1024]{2,1,0:T(8,128)(2,1)S(1)} %collective-permute-done), channel_id=1, source_target_pairs={{0,2},{2,4},{4,6},{6,8},{8,10},{10,12},{12,14},{14,0},{1,3},{3,5},... | collective-permute-start | bytes 3145736 | tf_op jit(solution)/shard_map/ppermute | solution.py:46
  64.2 1.0 copy-start.3
  65.2 26.2 %collective-permute-start.2 = (bf16[2,256,1024]{2,1,0:T(8,128)(2,1)S(1)}, bf16[2,256,1024]{2,1,0:T(8,128)(2,1)S(1)}, u32[]{:S(2)}, u32[]{:S(2)}) collective-permute-start(bf16[2,256,1024]{2,1,0:T(8,128)(2,1)S(1)} %collective-permute-done.1), channel_id=1, source_target_pairs={{0,2},{2,4},{4,6},{6,8},{8,10},{10,12},{12,14},{14,0},{1,3},{3,5},... | collective-permute-start | bytes 3145736 | tf_op jit(solution)/shard_map/ppermute | solution.py:46
  91.4 1.0 copy-start.5
  92.4 25.3 %collective-permute-start.3 = (bf16[2,256,1024]{2,1,0:T(8,128)(2,1)S(1)}, bf16[2,256,1024]{2,1,0:T(8,128)(2,1)S(1)}, u32[]{:S(2)}, u32[]{:S(2)}) collective-permute-start(bf16[2,256,1024]{2,1,0:T(8,128)(2,1)S(1)} %collective-permute-done.2), channel_id=1, source_target_pairs={{0,2},{2,4},{4,6},{6,8},{8,10},{10,12},{12,14},{14,0},{1,3},{3,5},... | collective-permute-start | bytes 3145736 | tf_op jit(solution)/shard_map/ppermute | solution.py:46
  117.7 1.0 copy-start.7
  118.7 24.5 %collective-permute-start.4 = (bf16[2,256,1024]{2,1,0:T(8,128)(2,1)S(1)}, bf16[2,256,1024]{2,1,0:T(8,128)(2,1)S(1)}, u32[]{:S(2)}, u32[]{:S(2)}) collective-permute-start(bf16[2,256,1024]{2,1,0:T(8,128)(2,1)S(1)} %collective-permute-done.3), channel_id=1, source_target_pairs={{0,2},{2,4},{4,6},{6,8},{8,10},{10,12},{12,14},{14,0},{1,3},{3,5},... | collective-permute-start | bytes 3145736 | tf_op jit(solution)/shard_map/ppermute | solution.py:46
  143.1 1.0 copy-start.9
  144.1 23.7 %collective-permute-start.5 = (bf16[2,256,1024]{2,1,0:T(8,128)(2,1)S(1)}, bf16[2,256,1024]{2,1,0:T(8,128)(2,1)}, u32[]{:S(2)}, u32[]{:S(2)}) collective-permute-start(bf16[2,256,1024]{2,1,0:T(8,128)(2,1)S(1)} %collective-permute-done.4), channel_id=1, source_target_pairs={{0,2},{2,4},{4,6},{6,8},{8,10},{10,12},{12,14},{14,0},{1,3},{3,5},... | collective-permute-start | bytes 3145736 | tf_op jit(solution)/shard_map/ppermute | solution.py:46
  167.8 23.1 %collective-permute-start.6 = (bf16[2,256,1024]{2,1,0:T(8,128)(2,1)}, bf16[2,256,1024]{2,1,0:T(8,128)(2,1)}, u32[]{:S(2)}, u32[]{:S(2)}) collective-permute-start(bf16[2,256,1024]{2,1,0:T(8,128)(2,1)} %collective-permute-done.5), channel_id=1, source_target_pairs={{0,2},{2,4},{4,6},{6,8},{8,10},{10,12},{12,14},{14,0},{1,3},{3,5},... | collective-permute-start | bytes 3145736 | tf_op jit(solution)/shard_map/ppermute | solution.py:46
  167.8 43.4 %copy-start.10 = (bf16[2,256,1024]{2,1,0:T(8,128)(2,1)S(1)}, bf16[2,256,1024]{2,1,0:T(8,128)(2,1)}, u32[]{:S(2)}) copy-start(bf16[2,256,1024]{2,1,0:T(8,128)(2,1)} %copy-done.9) | copy-start | bytes 3145732
  167.8 44.4 %copy-start.8 = (bf16[2,256,1024]{2,1,0:T(8,128)(2,1)S(1)}, bf16[2,256,1024]{2,1,0:T(8,128)(2,1)}, u32[]{:S(2)}) copy-start(bf16[2,256,1024]{2,1,0:T(8,128)(2,1)} %copy-done.7) | copy-start | bytes 3145732
  167.8 45.4 %copy-start.6 = (bf16[2,256,1024]{2,1,0:T(8,128)(2,1)S(1)}, bf16[2,256,1024]{2,1,0:T(8,128)(2,1)}, u32[]{:S(2)}) copy-start(bf16[2,256,1024]{2,1,0:T(8,128)(2,1)} %copy-done.5) | copy-start | bytes 3145732
  167.8 46.5 %copy-start.4 = (bf16[2,256,1024]{2,1,0:T(8,128)(2,1)S(1)}, bf16[2,256,1024]{2,1,0:T(8,128)(2,1)}, u32[]{:S(2)}) copy-start(bf16[2,256,1024]{2,1,0:T(8,128)(2,1)} %copy-done.3) | copy-start | bytes 3145732
  213.3 11.9 %copy-start.19 = (f32[2]{0:T(128)S(1)}, f32[2]{0:T(128)}, u32[]{:S(2)}) copy-start(f32[2]{0:T(128)} %param.10) | copy-start | bytes 28
  213.3 12.4 %copy-start.18 = (s32[512]{0:T(512)S(1)}, s32[512]{0:T(512)}, u32[]{:S(2)}) copy-start(s32[512]{0:T(512)} %param.15) | copy-start | bytes 6148
  213.3 13.1 %copy-start.15 = (f32[64]{0:T(128)S(1)}, f32[64]{0:T(128)}, u32[]{:S(2)}) copy-start(f32[64]{0:T(128)} %param.13) | copy-start | bytes 772
  301.4 25.1 %copy-start.11 = (f32[1024,512]{0,1:T(8,128)S(1)}, f32[1024,512]{0,1:T(8,128)}, u32[]{:S(2)}) copy-start(f32[1024,512]{0,1:T(8,128)} %get-tuple-element.11) | copy-start | bytes 6291460
  326.5 49.3 %copy-start.12 = (f32[512,64]{0,1:T(8,128)S(1)}, f32[512,64]{0,1:T(8,128)}, u32[]{:S(2)}) copy-start(f32[512,64]{0,1:T(8,128)} %get-tuple-element.13) | copy-start | bytes 393220
  326.5 49.3 %copy-start.13 = (f32[512,64]{0,1:T(8,128)S(1)}, f32[512,64]{0,1:T(8,128)}, u32[]{:S(2)}) copy-start(f32[512,64]{0,1:T(8,128)} %get-tuple-element.14) | copy-start | bytes 393220
  326.5 49.3 %copy-start.16 = (f32[2]{0:T(128)S(1)}, f32[2]{0:T(128)}, u32[]{:S(2)}) copy-start(f32[2]{0:T(128)} %param.11) | copy-start | bytes 28
  326.5 49.3 %copy-start.17 = (f32[2]{0:T(128)S(1)}, f32[2]{0:T(128)}, u32[]{:S(2)}) copy-start(f32[2]{0:T(128)} %integer_pow.13) | copy-start | bytes 28
  326.5 49.5 %copy-start.14 = (s32[512]{0:T(512)S(1)}, s32[512]{0:T(512)}, u32[]{:S(2)}) copy-start(s32[512]{0:T(512)} %param.14) | copy-start | bytes 6148
  326.5 53.9 %copy-start.1 = (f32[512]{0:T(512)S(1)}, f32[512]{0:T(512)}, u32[]{:S(2)}) copy-start(f32[512]{0:T(512)} %param.12) | copy-start | bytes 6148
Sparse Core Ops, SparseCore 0:
  225.3 26.1 all-gather.1
